TPU v7x, 32 devices: a whole 2x2x4 slice. The times are simulated.
32 devices in a mesh: samp: 16 (over z, y, x), tgt: 2 (over core).
Axes of the slice: x: 2, y: 2, z: 4, core: 2. Of those that a mesh axis runs over, the one named last changes fastest.
Arguments:
- samples: bfloat16 [3072, 128], P('samp'), may hold values from -6 to 6
- omega: bfloat16 [128, 4096], replicated, may hold values from -0.5 to 0.5
- phase: float32 [4096], replicated, may hold values from -3.140625 to 3.140625
- right_side: float32 [4096, 512], P('samp', 'tgt'), may hold values from -6 to 6
Outputs:
- weights: float32 [4096, 512], P('samp', 'tgt')
All inputs are finite; a program needn't handle non-finite values.
Results may differ from a plain program's by a relative error of at most 0.011.
The roundings to bfloat16 on the way count: a program that leaves them out, or rounds other values in their place, can miss the bound.
Values may be sent and summed in bfloat16 or wider, within the bound.
A program may use at most 128 MiB of HBM per device.

v0:
```python
import math
import jax
import jax.numpy as jnp
from jax import lax
from jax.sharding import PartitionSpec as P

ITERS = 2
ridge = 1.0


def precise_dot(left_matrix, right_matrix):
    return jnp.dot(left_matrix, right_matrix, precision=lax.Precision.HIGHEST)


def spd_solve(gram_matrix, rhs_matrix):
    factor = jnp.linalg.cholesky(gram_matrix)
    return jax.scipy.linalg.cho_solve((factor, True), rhs_matrix)


def cosine_block(samples, omega, phase, first_row, row_count):
    omega_cols = lax.dynamic_slice_in_dim(omega, first_row, row_count, 1)
    phase_cols = lax.dynamic_slice_in_dim(phase, first_row, row_count, 0)
    preact = jnp.dot(samples, omega_cols, preferred_element_type=jnp.float32) + phase_cols
    return jnp.cos(preact).astype(jnp.bfloat16)


def full_gram(stacked):
    summed = lax.psum(stacked, "samp")
    return lax.all_gather(summed, "tgt", axis=2, tiled=True)


def body(samples, omega, phase, right_side):
    feat_rows, col_count = right_side.shape
    samp_count = lax.axis_size("samp")
    feat_total = omega.shape[1]
    sample_total = samples.shape[0] * samp_count
    col_offset = lax.axis_index("tgt") * col_count
    store_block = math.gcd(feat_total, 512)
    stored = jnp.concatenate(
        [
            cosine_block(samples, omega, phase, index_block * store_block, store_block)
            for index_block in range(feat_total // store_block)
        ],
        axis=1,
    )

    def columns(first_row, row_count):
        return lax.dynamic_slice_in_dim(stored, first_row, row_count, 1)

    resid_all = lax.all_gather(right_side, "tgt", axis=1, tiled=True)
    direction_all = resid_all
    weight_own = jnp.zeros_like(right_side)
    gram_rr = full_gram(precise_dot(resid_all.T, right_side)[None])[0]
    for iteration in range(ITERS):
        direction_own = lax.dynamic_slice_in_dim(direction_all, col_offset, col_count, 1)
        initial = jnp.zeros((samples.shape[0], col_count), jnp.float32)
        shard_piece = lax.all_gather(direction_own.astype(jnp.bfloat16), "samp", axis=0, tiled=True)
        piece_rows = shard_piece.shape[0]
        block_size = math.gcd(piece_rows, 512)

        def project_one_block(index_block, acc_value):
            begin_row = index_block * block_size
            sub_piece = lax.dynamic_slice_in_dim(shard_piece, begin_row, block_size, 0)
            return acc_value + jnp.dot(
                columns(begin_row, block_size), sub_piece, preferred_element_type=jnp.float32
            )

        projected = lax.fori_loop(0, piece_rows // block_size, project_one_block, initial)
        proj_bf = projected.astype(jnp.bfloat16)
        transpose_row_count = feat_rows * lax.axis_size("samp")
        transpose_block_size = math.gcd(transpose_row_count, 512)

        def transpose_one_block(index_block, result):
            begin_row = index_block * transpose_block_size
            feats_block = columns(begin_row, transpose_block_size)
            block_term = lax.dot_general(
                feats_block, proj_bf, (((0,), (0,)), ((), ())), preferred_element_type=jnp.float32
            )
            return lax.dynamic_update_slice_in_dim(result, block_term, begin_row, 0)

        zero_rows = jnp.zeros((transpose_row_count, col_count), jnp.float32)
        summed_image = lax.psum_scatter(
            lax.fori_loop(
                0, transpose_row_count // transpose_block_size, transpose_one_block, zero_rows
            ),
            "samp",
            scatter_dimension=0,
            tiled=True,
        )
        image_own = summed_image / sample_total + ridge * direction_own
        image_all = lax.all_gather(image_own, "tgt", axis=1, tiled=True)
        gram_pq = full_gram(precise_dot(direction_all.T, image_own)[None])[0]
        alpha_coef = spd_solve(gram_pq, gram_rr)
        alpha_own = lax.dynamic_slice_in_dim(alpha_coef, col_offset, col_count, 1)
        weight_own = weight_own + precise_dot(direction_all, alpha_own)
        if iteration + 1 < ITERS:
            resid_all = resid_all - precise_dot(image_all, alpha_coef)
            resid_now = lax.dynamic_slice_in_dim(resid_all, col_offset, col_count, 1)
            gram_new = full_gram(precise_dot(resid_all.T, resid_now)[None])[0]
            beta_coef = spd_solve(gram_rr, gram_new)
            direction_all = resid_all + precise_dot(direction_all, beta_coef)
            gram_rr = gram_new
    return weight_own


def solution(mesh):
    placed = (P("samp", None), P(), P(), P("samp", "tgt"))
    return jax.shard_map(
        body, mesh=mesh, in_specs=placed, out_specs=P("samp", "tgt"), check_vma=False
    )
```

profile of v0, /device:TPU:0, one launch (start us, length us, event | category | flops | bytes accessed | tf_op | source)
XLA Modules:
  0.0 1215.1 jit_solution(10789328759363507932)
XLA Ops:
  6.5 2.6 all_gather.24
  10.7 2.3 fusion.20
  22.8 50.4 %all-gather.7.cloned.1.call-done = bf16[4096,256]{1,0:T(8,128)(2,1)} async-done(((bf16[256,256]{1,0:T(8,128)(2,1)}), bf16[4096,256]{1,0:T(8,128)(2,1)}) %all-gather.7.cloned.1.call-update) | async-done | bytes 2097168 | tf_op jit(solution)/shard_map/all_gather | solution.py:57
  73.3 9.8 while.62
  83.1 2.2 broadcast.164.clone
  85.3 8.6 while.60
  96.3 91.8 %reduce-scatter.3.cloned.1.call-done = f32[256,256]{1,0:T(8,128)} async-done(((f32[4096,256]{1,0:T(8,128)}), f32[256,256]{1,0:T(8,128)}) %reduce-scatter.3.cloned.1.call-update) | async-done | bytes 262160 | tf_op jit(solution)/shard_map/reduce_scatter | solution.py:82
  190.6 114.9 %all-reduce.10.cloned.1.call-done = (f32[1,512,256]{1,2,0:T(8,128)}, f32[1,512,256]{1,2,0:T(8,128)}) async-done(((f32[1,512,256]{1,2,0:T(8,128)}, f32[1,512,256]{1,2,0:T(8,128)}), (f32[1,512,256]{1,2,0:T(8,128)}, f32[1,512,256]{1,2,0:T(8,128)})) %all-reduce.10.cloned.1.call-update) | async-done | bytes 1048592 | tf_op jit(solution)/shard_map/psum | solution.py:28
  305.5 2.3 all_gather.28
  307.9 7.1 all-gather.9.cloned.1.call-done
  315.0 2.6 copy.5
  320.1 11.7 cholesky.374
  332.0 9.8 custom-call.35
  344.3 11.7 cholesky.393
  356.1 10.0 custom-call.36
  367.6 11.7 cholesky.414
  380.0 9.8 custom-call.37
  391.3 11.7 cholesky.431
  408.6 12.0 while.64
  409.3 2.3 bitcast_dynamic-update-slice_fusion.6
  412.3 2.3 bitcast_dynamic-update-slice_fusion.6
  415.3 2.3 bitcast_dynamic-update-slice_fusion.6
  418.3 2.3 bitcast_dynamic-update-slice_fusion.6
  420.6 39.3 %custom-call.38 = f32[4,128,128]{1,2,0:T(8,128)S(1)} custom-call(f32[4,128,128]{2,1,0:T(8,128)S(1)} %get-tuple-element.377), custom_call_target="InvertDiagBlocksLowerTriangular" | custom-call | tf_op jit(solution)/shard_map/jit(_cho_solve)/triangular_solve | solution.py:17
  460.0 2.7 copy.7
  475.0 11.7 cholesky.446
  487.5 10.8 custom-call.39
  502.1 12.5 %cholesky.465 = f32[128,128]{1,0:T(8,128)S(1)} custom-call(f32[128,128]{1,0:T(8,128)} %cholesky.603), custom_call_target="Cholesky" | custom-call | tf_op jit(solution)/shard_map/jit(cholesky)/cholesky | solution.py:16
  515.3 10.6 custom-call.40
  529.1 12.5 %cholesky.486 = f32[128,128]{1,0:T(8,128)} custom-call(f32[128,128]{1,0:T(8,128)S(1)} %cholesky.608), custom_call_target="Cholesky" | custom-call | tf_op jit(solution)/shard_map/jit(cholesky)/cholesky | solution.py:16
  543.1 10.4 custom-call.41
  555.9 12.3 %cholesky.503 = f32[128,128]{1,0:T(8,128)} custom-call(f32[128,128]{1,0:T(8,128)S(1)} %convolution_subtract_fusion.26), custom_call_target="Cholesky" | custom-call | tf_op jit(solution)/shard_map/jit(cholesky)/cholesky | solution.py:16
  568.2 2.3 convolution_subtract_fusion
  571.4 1.8 convolution_bitcast_fusion.2
  578.3 105.3 %all-reduce.6.cloned.1.call-done = f32[1,512,256]{2,1,0:T(8,128)} async-done(((f32[1,512,256]{2,1,0:T(8,128)}), f32[1,512,256]{2,1,0:T(8,128)}) %all-reduce.6.cloned.1.call-update) | async-done | bytes 524304 | tf_op jit(solution)/shard_map/psum | solution.py:28
  684.4 14.8 %while.65 = (s32[]{:T(128)}, f32[512,512]{1,0:T(8,128)}, s32[4,2]{0,1:T(2,128)S(1)}, f32[4,128,128]{2,1,0:T(8,128)}, s32[]{:T(128)}) while((s32[]{:T(128)}, f32[512,512]{1,0:T(8,128)}, s32[4,2]{0,1:T(2,128)S(1)}, f32[4,128,128]{2,1,0:T(8,128)}, s32[]{:T(128)}) %tuple.227), condition=%wide.while_cond.clone, body=%wide.while_body.clone.sunk | while | flops 2 | bytes 132705 | solution.py:17
  685.5 2.9 bitcast_dynamic-update-slice_fusion.7
  689.1 3.0 bitcast_dynamic-update-slice_fusion.7
  692.7 2.9 bitcast_dynamic-update-slice_fusion.7
  696.3 2.9 bitcast_dynamic-update-slice_fusion.7
  699.2 40.8 %custom-call.42 = f32[4,128,128]{1,2,0:T(8,128)} custom-call(f32[4,128,128]{2,1,0:T(8,128)} %get-tuple-element.378), custom_call_target="InvertDiagBlocksLowerTriangular" | custom-call | tf_op jit(solution)/shard_map/jit(_cho_solve)/triangular_solve | solution.py:17
  752.9 59.5 %all-gather.15.cloned.1.call-done = bf16[4096,256]{1,0:T(8,128)(2,1)} async-done(((bf16[256,256]{1,0:T(8,128)(2,1)}), bf16[4096,256]{1,0:T(8,128)(2,1)}) %all-gather.15.cloned.1.call-update) | async-done | bytes 2097168 | tf_op jit(solution)/shard_map/all_gather | solution.py:57
  812.4 9.8 while.63
  822.2 2.2 broadcast.164
  824.4 8.6 while.61
  833.1 94.1 %reduce-scatter.5.cloned.1.call-done = f32[256,256]{1,0:T(8,128)} async-done(((f32[4096,256]{1,0:T(8,128)}), f32[256,256]{1,0:T(8,128)}) %reduce-scatter.5.cloned.1.call-update) | async-done | bytes 262160 | tf_op jit(solution)/shard_map/reduce_scatter | solution.py:82
  927.2 2.4 convolution_bitcast_fusion
  929.9 111.0 %all-reduce.8.cloned.1.call-done = f32[1,512,256]{1,2,0:T(8,128)} async-done(((f32[1,512,256]{1,2,0:T(8,128)}), f32[1,512,256]{1,2,0:T(8,128)}) %all-reduce.8.cloned.1.call-update) | async-done | bytes 524304 | tf_op jit(solution)/shard_map/psum | solution.py:28
  1042.0 8.5 all-gather.17.cloned.1.call-done
  1050.5 2.6 copy.10
  1055.6 11.7 cholesky.518
  1067.5 9.8 custom-call.43
  1079.8 11.7 cholesky.537
  1092.9 10.0 custom-call.44
  1104.4 11.7 cholesky.558
  1116.8 9.8 custom-call.45
  1128.1 11.7 cholesky.575
  1144.4 11.5 while.66
  1145.0 2.3 bitcast_dynamic-update-slice_fusion.8
  1147.9 2.3 bitcast_dynamic-update-slice_fusion.8
  1150.8 2.3 bitcast_dynamic-update-slice_fusion.8
  1153.7 2.2 bitcast_dynamic-update-slice_fusion.8
  1155.9 39.3 %custom-call.46 = f32[4,128,128]{1,2,0:T(8,128)S(1)} custom-call(f32[4,128,128]{2,1,0:T(8,128)S(1)} %get-tuple-element.379), custom_call_target="InvertDiagBlocksLowerTriangular" | custom-call | tf_op jit(solution)/shard_map/jit(_cho_solve)/triangular_solve | solution.py:17
  1200.2 1.6 convolution_subtract_fusion.14
  (260 shorter events, 138.2 us)
Async XLA Ops:
  6.5 4.2 copy-start
  6.5 6.5 copy-start.26
  6.5 66.7 %all-gather.7.cloned.1.call-start = ((), (), s32[]{:S(2)}) async-start(), calls=%async_computation.2 | async-start | bytes 2228224 | tf_op jit(solution)/shard_map/all_gather | solution.py:57
  9.9 178.2 %reduce-scatter.3.cloned.1.call-start = ((), (), s32[]{:S(2)}) async-start(), calls=%async_computation.3 | async-start | bytes 4456448 | tf_op jit(solution)/shard_map/reduce_scatter | solution.py:82
  93.9 0.9 copy-start.19
  93.9 211.5 %all-reduce.10.cloned.1.call-start = ((), (), s32[]{:S(2)}) async-start(), calls=%async_computation.12 | async-start | bytes 2097152 | tf_op jit(solution)/shard_map/psum | solution.py:28
  190.5 124.4 %all-gather.9.cloned.1.call-start = ((), (), s32[]{:S(2)}) async-start(), calls=%async_computation.4 | async-start | bytes 1572864 | tf_op jit(solution)/shard_map/all_gather | solution.py:29
  305.5 154.5 %all-gather.11.cloned.1.call-start = ((), (), s32[]{:S(2)}) async-start(), calls=%async_computation.5 | async-start | bytes 1572864 | tf_op jit(solution)/shard_map/all_gather | solution.py:29
  307.8 375.8 %all-reduce.6.cloned.1.call-start = ((), (), s32[]{:S(2)}) async-start(), calls=%async_computation.6 | async-start | bytes 1048576 | tf_op jit(solution)/shard_map/psum | solution.py:28
  315.0 2.7 copy-start.9
  319.1 1.0 copy-start.15
  459.9 7.9 copy-start.20
  460.0 2.7 copy-start.1
  462.6 2.3 copy-start.7
  468.2 3.4 copy-start.21
  471.2 1.6 copy-start.2
  471.7 2.2 copy-start.10
  472.0 2.0 copy-start.12
  474.1 1.0 copy-start.16
  500.8 0.7 copy-start.23
  528.4 0.7 copy-start.24
  568.2 7.6 copy-start.25
  570.6 0.8 copy-start.4
  573.2 166.8 %all-gather.13.cloned.1.call-start = ((), (), s32[]{:S(2)}) async-start(), calls=%async_computation.7 | async-start | bytes 1572864 | tf_op jit(solution)/shard_map/all_gather | solution.py:29
  683.6 128.7 %all-gather.15.cloned.1.call-start = ((), (), s32[]{:S(2)}) async-start(), calls=%async_computation.8 | async-start | bytes 2228224 | tf_op jit(solution)/shard_map/all_gather | solution.py:57
  699.2 44.9 %copy-start.6 = (f32[512,512]{1,0:T(8,128)S(1)}, f32[512,512]{1,0:T(8,128)}, u32[]{:S(2)}) copy-start(f32[512,512]{1,0:T(8,128)} %get-tuple-element.842) | copy-start | bytes 3145732
  740.0 5.5 copy-start.22
  749.6 1.4 copy-start.5
  752.8 174.4 %reduce-scatter.5.cloned.1.call-start = ((), (), s32[]{:S(2)}) async-start(), calls=%async_computation.9 | async-start | bytes 4456448 | tf_op jit(solution)/shard_map/reduce_scatter | solution.py:82
  833.0 207.9 %copy-start.3 = (f32[128,512]{1,0:T(8,128)S(1)}, f32[128,512]{1,0:T(8,128)}, u32[]{:S(2)}) copy-start(f32[128,512]{1,0:T(8,128)} %copy-done.2) | copy-start | bytes 786436
  833.0 207.9 %copy-start.13 = (f32[128,512]{1,0:T(8,128)S(1)}, f32[128,512]{1,0:T(8,128)}, u32[]{:S(2)}) copy-start(f32[128,512]{1,0:T(8,128)} %copy-done.12) | copy-start | bytes 786436
  833.0 207.9 %copy-start.18 = (f32[128,512]{1,0:T(8,128)S(1)}, f32[128,512]{1,0:T(8,128)}, u32[]{:S(2)}) copy-start(f32[128,512]{1,0:T(8,128)} %fusion.170) | copy-start | bytes 786436
  833.0 207.9 %all-reduce.8.cloned.1.call-start = ((), (), s32[]{:S(2)}) async-start(), calls=%async_computation.10 | async-start | bytes 1048576 | tf_op jit(solution)/shard_map/psum | solution.py:28
  929.7 120.8 %all-gather.17.cloned.1.call-start = ((), (), s32[]{:S(2)}) async-start(), calls=%async_computation.11 | async-start | bytes 1572864 | tf_op jit(solution)/shard_map/all_gather | solution.py:29
  1050.5 2.7 copy-start.11
  1054.6 1.0 copy-start.14
  1155.9 42.5 %copy-start.8 = (f32[512,512]{1,0:T(8,128)S(1)}, f32[512,512]{1,0:T(8,128)}, u32[]{:S(2)}) copy-start(f32[512,512]{1,0:T(8,128)} %get-tuple-element.844) | copy-start | bytes 3145732
  1204.9 1.4 copy-start.17
Sparse Core Ops, SparseCore 0:
  10.1 63.1 all-gather.6
  94.0 94.0 reduce-scatter.2
  193.4 111.9 all-reduce.9
  306.8 8.0 all-gather.8
  316.4 10.1 all-gather.10
  573.3 110.2 all-reduce.5
  685.2 8.0 all-gather.12
  752.9 59.3 all-gather.14
  833.1 94.0 reduce-scatter.4
  932.2 108.6 all-reduce.7
  1042.4 8.0 all-gather.16
where the time goes:
time: 1230 us; the launch traced here: 1220 us
  waiting for transfers between devices  643 us (52%)
  other arithmetic  372 us (30%)
  matrix products  111 us (9%)
  local copies, waits for them, and re-layouts  60.6 us (5%)
  between operations  22.3 us (2%)
    psum x3, waiting for transfers between devices, full_gram(): summed = lax.psum(stacked, 'samp')  331 us
    another operation x43, other arithmetic, spd_solve(): factor = jnp.linalg.cholesky(gram_matrix)  243 us
    reduce_scatter x2, waiting for transfers between devices, body(): lax.psum_scatter(lax.fori_loop(0, transpose_row_count // transpose_block_...  186 us
    another operation x8, other arithmetic, spd_solve(): return jax.scipy.linalg.cho_solve((factor, True), rhs_matrix)  124 us
    all_gather x2, waiting for transfers between devices, body(): lax.all_gather(direction_own.astype(jnp.bfloat16), 'samp', axis=0, tiled=...  110 us
    another operation x40, local copies, waits for them, and re-layouts, spd_solve(): return jax.scipy.linalg.cho_solve((factor, True), rhs_matrix)  38.5 us
    another operation x42, matrix products, spd_solve(): return jax.scipy.linalg.cho_solve((factor, True), rhs_matrix)  31.8 us
  transfers between devices with their start and end apart: 11, of which 9 were waited for; matrix products, arithmetic and copies ran while one was open for 18% of the time, Pallas kernels for 0%

commit v1 on v0

--- a/solution.py
+++ b/solution.py
@@ -6,6 +6,25 @@
 
 ITERS = 2
 ridge = 1.0
+
+
+def laid_out(blocks, dim):
+    blocks = jnp.moveaxis(blocks, 0, dim)
+    lengths = blocks.shape
+    return blocks.reshape(*lengths[:dim], lengths[dim] * lengths[dim + 1], *lengths[dim + 2 :])
+
+
+def grow_blocks(value, axis):
+    size, index = (lax.axis_size(axis), lax.axis_index(axis))
+    blocks, stride = (value[None], 1)
+    while stride < size:
+        partner_block = lax.ppermute(blocks, axis, [(i, i ^ stride) for i in range(size)])
+        low = index & stride == 0
+        blocks = jnp.concatenate(
+            [jnp.where(low, blocks, partner_block), jnp.where(low, partner_block, blocks)]
+        )
+        stride *= 2
+    return blocks
 
 
 def precise_dot(left_matrix, right_matrix):
@@ -54,7 +73,8 @@
     for iteration in range(ITERS):
         direction_own = lax.dynamic_slice_in_dim(direction_all, col_offset, col_count, 1)
         initial = jnp.zeros((samples.shape[0], col_count), jnp.float32)
-        shard_piece = lax.all_gather(direction_own.astype(jnp.bfloat16), "samp", axis=0, tiled=True)
+        x = direction_own.astype(jnp.bfloat16)
+        shard_piece = laid_out(grow_blocks(x, "samp"), 0)
         piece_rows = shard_piece.shape[0]
         block_size = math.gcd(piece_rows, 512)
 

time: 1230 us -> 1250 us (1.016)
  starting transfers between devices: 0.93 us -> 15.6 us
    all_gather x2 -> x0, waiting for transfers between devices: 110 us -> none  [body(): lax.all_gather(direction_own.astype(jnp.bfloat16), 'samp', axis=0, tiled=...]
    ppermute x0 -> x8, waiting for transfers between devices: none -> 104 us  [grow_blocks(): lax.ppermute(blocks, axis, [(i, i ^ stride) for i in range(size)])]
    ppermute x0 -> x8, starting transfers between devices: none -> 15.1 us  [grow_blocks(): lax.ppermute(blocks, axis, [(i, i ^ stride) for i in range(size)])]
  transfers between devices with their start and end apart: 11 -> 17, of which waited for: 9 -> 15; matrix products, arithmetic and copies ran while one was open for 18% -> 18% of each run, Pallas kernels for 0% -> 0%
where the time goes in v1:
time: 1250 us; the launch traced here: 1240 us
  waiting for transfers between devices  640 us (51%)
  other arithmetic  382 us (31%)
  matrix products  117 us (9%)
  local copies, waits for them, and re-layouts  58.9 us (5%)
  between operations  22.5 us (2%)
  starting transfers between devices  15.6 us (1%)
    psum x3, waiting for transfers between devices, full_gram(): summed = lax.psum(stacked, 'samp')  331 us
    another operation x43, other arithmetic, spd_solve(): factor = jnp.linalg.cholesky(gram_matrix)  243 us
    reduce_scatter x2, waiting for transfers between devices, body(): lax.psum_scatter(lax.fori_loop(0, transpose_row_count // transpose_block_...  188 us
    another operation x8, other arithmetic, spd_solve(): return jax.scipy.linalg.cho_solve((factor, True), rhs_matrix)  124 us
    ppermute x8, waiting for transfers between devices, grow_blocks(): lax.ppermute(blocks, axis, [(i, i ^ stride) for i in range(size)])  104 us
    another operation x40, local copies, waits for them, and re-layouts, spd_solve(): return jax.scipy.linalg.cho_solve((factor, True), rhs_matrix)  37.7 us
    another operation x42, matrix products, spd_solve(): return jax.scipy.linalg.cho_solve((factor, True), rhs_matrix)  31.8 us
  transfers between devices with their start and end apart: 17, of which 15 were waited for; matrix products, arithmetic and copies ran while one was open for 18% of the time, Pallas kernels for 0%

profile of v1, /device:TPU:0, one launch (start us, length us, event | category | flops | bytes accessed | tf_op | source)
XLA Modules:
  0.0 1241.8 jit_solution(13881982140511247523)
XLA Ops:
  6.5 2.6 all_gather.18
  9.2 2.9 collective-permute-start
  12.1 3.8 collective-permute-done
  17.9 6.0 collective-permute-done.1
  27.9 2.3 fusion.22
  30.2 2.3 fusion.24
  32.5 4.2 collective-permute-done.2
  43.6 2.3 fusion.28
  45.9 2.3 fusion.30
  48.2 2.3 fusion.32
  52.8 32.8 %collective-permute-done.3 = bf16[8,256,256]{2,1,0:T(8,128)(2,1)} collective-permute-done((bf16[8,256,256]{2,1,0:T(8,128)(2,1)}, bf16[8,256,256]{2,1,0:T(8,128)(2,1)}, u32[]{:S(2)}, u32[]{:S(2)}) %collective-permute-start.3) | collective-permute-done | bytes 1048608 | tf_op jit(solution)/shard_map/ppermute | solution.py:21
  88.9 9.8 while.62
  100.9 8.7 while.60
  112.0 93.5 %reduce-scatter.3.cloned.1.call-done = f32[256,256]{1,0:T(8,128)} async-done(((f32[4096,256]{1,0:T(8,128)}), f32[256,256]{1,0:T(8,128)}) %reduce-scatter.3.cloned.1.call-update) | async-done | bytes 262160 | tf_op jit(solution)/shard_map/reduce_scatter | solution.py:102
  208.0 114.9 %all-reduce.10.cloned.1.call-done = (f32[1,512,256]{1,2,0:T(8,128)}, f32[1,512,256]{1,2,0:T(8,128)}) async-done(((f32[1,512,256]{1,2,0:T(8,128)}, f32[1,512,256]{1,2,0:T(8,128)}), (f32[1,512,256]{1,2,0:T(8,128)}, f32[1,512,256]{1,2,0:T(8,128)})) %all-reduce.10.cloned.1.call-update) | async-done | bytes 1048592 | tf_op jit(solution)/shard_map/psum | solution.py:47
  322.9 2.3 all_gather.21
  325.3 7.2 all-gather.5.cloned.1.call-done
  332.6 2.6 copy.5
  337.6 11.7 cholesky.374
  349.5 9.8 custom-call.35
  361.9 11.7 cholesky.393
  373.6 10.0 custom-call.36
  385.2 11.7 cholesky.414
  397.6 9.8 custom-call.37
  408.8 11.7 cholesky.431
  426.0 11.5 while.64
  437.5 39.3 %custom-call.38 = f32[4,128,128]{1,2,0:T(8,128)S(1)} custom-call(f32[4,128,128]{2,1,0:T(8,128)S(1)} %get-tuple-element.377), custom_call_target="InvertDiagBlocksLowerTriangular" | custom-call | tf_op jit(solution)/shard_map/jit(_cho_solve)/triangular_solve | solution.py:36
  476.9 2.6 copy.7
  491.9 11.7 cholesky.446
  504.4 10.8 custom-call.39
  519.1 12.5 %cholesky.465 = f32[128,128]{1,0:T(8,128)S(1)} custom-call(f32[128,128]{1,0:T(8,128)} %cholesky.603), custom_call_target="Cholesky" | custom-call | tf_op jit(solution)/shard_map/jit(cholesky)/cholesky | solution.py:35
  532.3 10.6 custom-call.40
  546.1 12.5 %cholesky.486 = f32[128,128]{1,0:T(8,128)} custom-call(f32[128,128]{1,0:T(8,128)S(1)} %cholesky.608), custom_call_target="Cholesky" | custom-call | tf_op jit(solution)/shard_map/jit(cholesky)/cholesky | solution.py:35
  560.1 10.4 custom-call.41
  572.9 12.3 cholesky.503
  585.2 2.3 convolution_subtract_fusion
  595.4 105.3 %all-reduce.6.cloned.1.call-done = f32[1,512,256]{2,1,0:T(8,128)} async-done(((f32[1,512,256]{2,1,0:T(8,128)}), f32[1,512,256]{2,1,0:T(8,128)}) %all-reduce.6.cloned.1.call-update) | async-done | bytes 524304 | tf_op jit(solution)/shard_map/psum | solution.py:47
  701.5 14.3 %while.65 = (s32[]{:T(128)}, f32[512,512]{1,0:T(8,128)}, s32[4,2]{0,1:T(2,128)S(1)}, f32[4,128,128]{2,1,0:T(8,128)}, s32[]{:T(128)}) while((s32[]{:T(128)}, f32[512,512]{1,0:T(8,128)}, s32[4,2]{0,1:T(2,128)S(1)}, f32[4,128,128]{2,1,0:T(8,128)}, s32[]{:T(128)}) %tuple.233), condition=%wide.while_cond.clone, body=%wide.while_body.clone.sunk | while | flops 2 | bytes 132705 | solution.py:36
  702.5 2.9 bitcast_dynamic-update-slice_fusion.7
  706.0 2.9 bitcast_dynamic-update-slice_fusion.7
  709.5 2.9 bitcast_dynamic-update-slice_fusion.7
  713.0 2.8 bitcast_dynamic-update-slice_fusion.7
  715.8 40.8 %custom-call.42 = f32[4,128,128]{1,2,0:T(8,128)} custom-call(f32[4,128,128]{2,1,0:T(8,128)} %get-tuple-element.378), custom_call_target="InvertDiagBlocksLowerTriangular" | custom-call | tf_op jit(solution)/shard_map/jit(_cho_solve)/triangular_solve | solution.py:36
  770.3 3.5 collective-permute-done.4
  775.5 4.9 collective-permute-done.5
  781.3 8.6 collective-permute-done.6
  791.9 2.5 collective-permute-start.7
  794.4 40.6 %collective-permute-done.7 = bf16[8,256,256]{2,1,0:T(8,128)(2,1)} collective-permute-done((bf16[8,256,256]{2,1,0:T(8,128)(2,1)}, bf16[8,256,256]{2,1,0:T(8,128)(2,1)}, u32[]{:S(2)}, u32[]{:S(2)}) %collective-permute-start.7) | collective-permute-done | bytes 1048608 | tf_op jit(solution)/shard_map/ppermute | solution.py:21
  838.2 9.8 while.63
  850.2 8.7 while.61
  859.0 94.5 %reduce-scatter.5.cloned.1.call-done = f32[256,256]{1,0:T(8,128)} async-done(((f32[4096,256]{1,0:T(8,128)}), f32[256,256]{1,0:T(8,128)}) %reduce-scatter.5.cloned.1.call-update) | async-done | bytes 262160 | tf_op jit(solution)/shard_map/reduce_scatter | solution.py:102
  953.5 2.4 convolution_bitcast_fusion
  956.2 111.1 %all-reduce.8.cloned.1.call-done = f32[1,512,256]{1,2,0:T(8,128)} async-done(((f32[1,512,256]{1,2,0:T(8,128)}), f32[1,512,256]{1,2,0:T(8,128)}) %all-reduce.8.cloned.1.call-update) | async-done | bytes 524304 | tf_op jit(solution)/shard_map/psum | solution.py:47
  1068.4 8.5 all-gather.11.cloned.1.call-done
  1076.9 2.6 copy.9
  1082.0 11.7 cholesky.518
  1093.9 9.8 custom-call.43
  1106.2 11.7 cholesky.537
  1119.3 10.0 custom-call.44
  1130.9 11.7 cholesky.558
  1143.3 9.8 custom-call.45
  1154.6 11.7 cholesky.575
  1170.9 11.7 while.66
  1182.6 39.3 %custom-call.46 = f32[4,128,128]{1,2,0:T(8,128)S(1)} custom-call(f32[4,128,128]{2,1,0:T(8,128)S(1)} %get-tuple-element.379), custom_call_target="InvertDiagBlocksLowerTriangular" | custom-call | tf_op jit(solution)/shard_map/jit(_cho_solve)/triangular_solve | solution.py:36
  (296 shorter events, 179.6 us)
Async XLA Ops:
  6.5 19.1 %copy-start = (bf16[192,128]{1,0:T(8,128)(2,1)S(1)}, bf16[192,128]{1,0:T(8,128)(2,1)}, u32[]{:S(2)}) copy-start(bf16[192,128]{1,0:T(8,128)(2,1)} %param.15) | copy-start | bytes 147460
  6.5 11.3 copy-start.31
  6.5 199.0 %reduce-scatter.3.cloned.1.call-start = ((), (), s32[]{:S(2)}) async-start(), calls=%async_computation.2 | async-start | bytes 4456448 | tf_op jit(solution)/shard_map/reduce_scatter | solution.py:102
  9.2 6.7 collective-permute-start
  16.0 7.8 collective-permute-start.1
  23.9 1.7 copy-start.21
  23.9 1.7 copy-start.22
  24.0 12.7 %collective-permute-start.2 = (bf16[4,256,256]{2,1,0:T(8,128)(2,1)S(1)}, bf16[4,256,256]{2,1,0:T(8,128)(2,1)}, u32[]{:S(2)}, u32[]{:S(2)}) collective-permute-start(bf16[4,256,256]{2,1,0:T(8,128)(2,1)S(1)} %pad_maximum_fusion.5), channel_id=1, source_target_pairs={{0,8},{2,10},{4,12},{6,14},{8,0},{10,2},{12,4},{14,6},{16,24},{18,... | collective-permute-start | bytes 1572872 | tf_op jit(solution)/shard_map/ppermute | solution.py:21
  39.0 46.6 %collective-permute-start.3 = (bf16[8,256,256]{2,1,0:T(8,128)(2,1)}, bf16[8,256,256]{2,1,0:T(8,128)(2,1)}, u32[]{:S(2)}, u32[]{:S(2)}) collective-permute-start(bf16[8,256,256]{2,1,0:T(8,128)(2,1)} %pad_maximum_fusion.2), channel_id=1, source_target_pairs={{0,16},{2,18},{4,20},{6,22},{8,24},{10,26},{12,28},{14,30},{16,0},... | collective-permute-start | bytes 3145736 | tf_op jit(solution)/shard_map/ppermute | solution.py:21
  109.6 0.9 copy-start.24
  109.6 213.3 %all-reduce.10.cloned.1.call-start = ((), (), s32[]{:S(2)}) async-start(), calls=%async_computation.10 | async-start | bytes 2097152 | tf_op jit(solution)/shard_map/psum | solution.py:47
  207.9 124.6 %all-gather.5.cloned.1.call-start = ((), (), s32[]{:S(2)}) async-start(), calls=%async_computation.3 | async-start | bytes 1572864 | tf_op jit(solution)/shard_map/all_gather | solution.py:48
  322.9 154.0 %all-gather.7.cloned.1.call-start = ((), (), s32[]{:S(2)}) async-start(), calls=%async_computation.4 | async-start | bytes 1572864 | tf_op jit(solution)/shard_map/all_gather | solution.py:48
  325.3 375.4 %all-reduce.6.cloned.1.call-start = ((), (), s32[]{:S(2)}) async-start(), calls=%async_computation.5 | async-start | bytes 1048576 | tf_op jit(solution)/shard_map/psum | solution.py:47
  332.6 2.6 copy-start.12
  336.6 1.0 copy-start.18
  476.8 7.9 copy-start.25
  476.9 2.6 copy-start.2
  479.5 2.3 copy-start.10
  485.1 3.4 copy-start.26
  488.1 1.5 copy-start.3
  488.6 2.2 copy-start.13
  488.9 2.0 copy-start.15
  491.0 1.0 copy-start.19
  517.7 0.7 copy-start.28
  545.4 0.7 copy-start.29
  585.2 7.7 copy-start.30
  587.6 0.8 copy-start.5
  590.2 166.4 %all-gather.9.cloned.1.call-start = ((), (), s32[]{:S(2)}) async-start(), calls=%async_computation.6 | async-start | bytes 1572864 | tf_op jit(solution)/shard_map/all_gather | solution.py:48
  700.7 252.8 %reduce-scatter.5.cloned.1.call-start = ((), (), s32[]{:S(2)}) async-start(), calls=%async_computation.7 | async-start | bytes 4456448 | tf_op jit(solution)/shard_map/reduce_scatter | solution.py:102
  715.8 44.9 %copy-start.9 = (f32[512,512]{1,0:T(8,128)S(1)}, f32[512,512]{1,0:T(8,128)}, u32[]{:S(2)}) copy-start(f32[512,512]{1,0:T(8,128)} %get-tuple-element.856) | copy-start | bytes 3145732
  756.7 5.5 copy-start.27
  766.2 1.4 copy-start.6
  768.8 5.0 collective-permute-start.4
  773.9 6.4 collective-permute-start.5
  780.5 9.4 collective-permute-start.6
  790.0 0.8 copy-start.7
  790.0 1.9 copy-start.8
  791.9 43.1 %collective-permute-start.7 = (bf16[8,256,256]{2,1,0:T(8,128)(2,1)}, bf16[8,256,256]{2,1,0:T(8,128)(2,1)}, u32[]{:S(2)}, u32[]{:S(2)}) collective-permute-start(bf16[8,256,256]{2,1,0:T(8,128)(2,1)} %pad_maximum_fusion.4), channel_id=1, source_target_pairs={{0,16},{2,18},{4,20},{6,22},{8,24},{10,26},{12,28},{14,30},{16,0},... | collective-permute-start | bytes 3145736 | tf_op jit(solution)/shard_map/ppermute | solution.py:21
  858.9 208.4 %copy-start.4 = (f32[128,512]{1,0:T(8,128)S(1)}, f32[128,512]{1,0:T(8,128)}, u32[]{:S(2)}) copy-start(f32[128,512]{1,0:T(8,128)} %copy-done.3) | copy-start | bytes 786436
  858.9 208.4 %copy-start.16 = (f32[128,512]{1,0:T(8,128)S(1)}, f32[128,512]{1,0:T(8,128)}, u32[]{:S(2)}) copy-start(f32[128,512]{1,0:T(8,128)} %copy-done.15) | copy-start | bytes 786436
  858.9 208.4 %copy-start.23 = (f32[128,512]{1,0:T(8,128)S(1)}, f32[128,512]{1,0:T(8,128)}, u32[]{:S(2)}) copy-start(f32[128,512]{1,0:T(8,128)} %fusion.172) | copy-start | bytes 786436
  859.0 208.4 %all-reduce.8.cloned.1.call-start = ((), (), s32[]{:S(2)}) async-start(), calls=%async_computation.8 | async-start | bytes 1048576 | tf_op jit(solution)/shard_map/psum | solution.py:47
  956.0 120.9 %all-gather.11.cloned.1.call-start = ((), (), s32[]{:S(2)}) async-start(), calls=%async_computation.9 | async-start | bytes 1572864 | tf_op jit(solution)/shard_map/all_gather | solution.py:48
  1076.9 2.6 copy-start.14
  1081.0 1.0 copy-start.17
  1182.6 42.5 %copy-start.11 = (f32[512,512]{1,0:T(8,128)S(1)}, f32[512,512]{1,0:T(8,128)}, u32[]{:S(2)}) copy-start(f32[512,512]{1,0:T(8,128)} %get-tuple-element.858) | copy-start | bytes 3145732
  1231.6 1.4 copy-start.20
  1231.6 3.3 copy-start.1
Sparse Core Ops, SparseCore 0:
  109.7 95.7 reduce-scatter.2
  210.8 111.9 all-reduce.9
  324.4 8.0 all-gather.4
  333.9 10.2 all-gather.6
  590.3 110.3 all-reduce.5
  702.1 8.0 all-gather.8
  859.0 94.4 reduce-scatter.4
  958.7 108.5 all-reduce.7
  1068.9 8.0 all-gather.10
